TPU v7x, 32 devices: a whole 2x2x4 slice. The times are simulated.
32 devices in a mesh: groups: 2 (over y), blk: 4 (over z), ulysses: 2 (over x), cfg: 2 (over core).
Axes of the slice: x: 2, y: 2, z: 4, core: 2. Of those that a mesh axis runs over, the one named last changes fastest.
Arguments:
- img_tokens: bfloat16 [2, 2, 512, 2432], P('cfg', 'groups', ('blk', 'ulysses')), parts along dimension 1, may hold values from -72 to 72
- text_tokens: bfloat16 [2, 2, 48, 2432], P('cfg', 'groups', ('blk', 'ulysses')), parts along dimension 1, may hold values from -6 to 6
- text_lengths: int32 [2, 2], P('cfg', 'groups'), parts along dimension 1, may hold values from 12 to 48
- timestep: int32 [2], P('groups'), parts along dimension 0, may hold values from 0 to 999
- pooled: float32 [2, 2, 2432], P(None, 'groups'), parts along dimension 1, may hold values from -6 to 6
- time_weight: bfloat16 [256, 2432], replicated, may hold values from -0.375 to 0.375
- time_second: bfloat16 [2432, 2432], P(None, ('blk', 'ulysses', 'cfg')), may hold values from -0.125 to 0.125
- mod_weight: bfloat16 [2432, 24320], P(None, ('blk', 'ulysses', 'cfg')), may hold values from -0.125 to 0.125
- proj_weight: bfloat16 [5, 2432, 2048], P(None, None, ('ulysses', 'cfg')), may hold values from -0.125 to 0.125
- out_weight: bfloat16 [2048, 2432], P(('ulysses', 'cfg')), may hold values from -0.125 to 0.125
- expand_weight: bfloat16 [2432, 7168], P('blk', ('ulysses', 'cfg')), may hold values from -0.125 to 0.125
- reduce_weight: bfloat16 [7168, 2432], P(('ulysses', 'cfg'), 'blk'), may hold values from -0.0625 to 0.0625
- qk_gain: float32 [3, 64], replicated, may hold values from 0.5 to 10
- final_weight: bfloat16 [2432, 64], replicated, may hold values from -0.125 to 0.125
Outputs:
- guided: float32 [2, 16, 16, 128], P('groups', None, ('blk', 'ulysses', 'cfg')), parts along dimension 0
There are 2 independent parts, one for each index of `groups`. A program takes and returns all parts, laid end to end along the dimension named above; an argument that names none is the same for every part. Nothing has to cross between parts.
All inputs are finite; a program needn't handle non-finite values.
Results may differ from a plain program's by a relative error of at most 0.011.
The roundings to bfloat16 on the way count: a program that leaves them out, or rounds other values in their place, can miss the bound.
Values may be sent and summed in bfloat16 or wider, within the bound.
A program may use at most 192 MiB of HBM per device.

v0:
```python
import math
import jax
import jax.numpy as jnp
from jax import lax
from jax.sharding import PartitionSpec as P

GUIDANCE = 3.5
LN_EPS = 1e-06
RMS_EPS = 1e-06
NEG_FILL = -1e30
block_keys = 512


def from_partner(value, axis, stride):
    mask = 2**stride
    pairs = [(source, source ^ mask) for source in range(lax.axis_size(axis))]
    return lax.ppermute(value, axis, pairs)


def sinusoid(timestep, feature_count):
    half_width = feature_count // 2
    frequency = jnp.exp(-math.log(10000.0) * jnp.arange(half_width, dtype=jnp.float32) / half_width)
    angles = timestep.astype(jnp.float32)[:, None] * frequency[None, :]
    return jnp.concatenate([jnp.cos(angles), jnp.sin(angles)], axis=1)


def layer_norm(values):
    average = jnp.mean(values, axis=-1, keepdims=True)
    centred = values - average
    variance = jnp.mean(centred * centred, axis=-1, keepdims=True)
    return centred * lax.rsqrt(variance + LN_EPS)


def modulate(values, shift, scale):
    return (layer_norm(values.astype(jnp.float32)) * (1.0 + scale) + shift).astype(jnp.bfloat16)


def rms_heads(values, gain):
    head_size = gain.shape[0]
    shaped = values.reshape(values.shape[:-1] + (values.shape[-1] // head_size, head_size))
    inverse = lax.rsqrt(jnp.mean(shaped * shaped, axis=-1, keepdims=True) + RMS_EPS)
    return (shaped * inverse * gain).reshape(values.shape).astype(jnp.bfloat16)


def finish(img_proj, txt_proj, gain_rows):
    img_set = jnp.stack(
        [
            rms_heads(img_proj[0], gain_rows[0]),
            rms_heads(img_proj[1], gain_rows[1]),
            img_proj[2].astype(jnp.bfloat16),
        ]
    )
    txt_set = jnp.stack([rms_heads(txt_proj[0], gain_rows[2]), txt_proj[1].astype(jnp.bfloat16)])
    return (img_set, txt_set)


def attend(state_now, query_heads, key_rows, value_rows, usable, scale):
    running_max, running_total, running_sum = state_now
    prompts, query_count, head_count, head_size = query_heads.shape
    key_count = key_rows.shape[1]
    key_heads = key_rows.reshape(prompts, key_count, head_count, head_size)
    value_heads = value_rows.reshape(prompts, key_count, head_count, head_size)
    scores = (
        jnp.einsum("pqhd,pkhd->phqk", query_heads, key_heads, preferred_element_type=jnp.float32)
        * scale
    )
    allowed = usable[:, None, None, :]
    block_max = jnp.max(jnp.where(allowed, scores, NEG_FILL), axis=3)
    new_max = jnp.maximum(running_max, block_max)
    weights = jnp.where(allowed, jnp.exp(scores - new_max[..., None]), 0.0)
    factor = jnp.exp(running_max - new_max)
    running_total = running_total * factor + jnp.sum(weights, axis=3)
    update = jnp.einsum(
        "phqk,pkhd->pqhd",
        weights.astype(jnp.bfloat16),
        value_heads,
        preferred_element_type=jnp.float32,
    )
    running_sum = running_sum * factor.transpose(0, 2, 1)[..., None] + update
    return (new_max, running_total, running_sum)


def attend_rows(state_now, query_heads, key_value, usable, scale):
    key_count = key_value.shape[2]
    for first_key in range(0, key_count, block_keys):
        last_key = min(first_key + block_keys, key_count)
        state_now = attend(
            state_now,
            query_heads,
            key_value[0, :, first_key:last_key],
            key_value[1, :, first_key:last_key],
            usable[:, first_key:last_key],
            scale,
        )
    return state_now


def make_fold(query_heads, lengths, img_span, txt_span, scale):
    span = img_span + txt_span

    def fold(state_now, kv_piece, first_row):
        key_count = kv_piece.shape[2]
        positions = jnp.arange(key_count, dtype=jnp.int32)
        shard_index = positions // span
        offset = positions - shard_index * span
        text_slot = offset - img_span
        usable = (offset < img_span)[None, :] | (text_slot[None, :] < lengths[:, None])
        return attend_rows(state_now, query_heads, kv_piece, usable, scale)

    return fold


def body(
    img_tokens,
    text_tokens,
    text_lengths,
    timestep,
    pooled,
    time_weight,
    time_second,
    mod_weight,
    proj_weight,
    out_weight,
    expand_weight,
    reduce_weight,
    qk_gain,
    final_weight,
):
    model_width = img_tokens.shape[3]
    prompts = img_tokens.shape[1]
    head_size = qk_gain.shape[1]
    branch = lax.axis_index("cfg")
    sinusoid_rows = sinusoid(timestep, time_weight.shape[0]).astype(jnp.bfloat16)
    time_hidden = jax.nn.silu(
        jnp.dot(sinusoid_rows, time_weight, preferred_element_type=jnp.float32)
    ).astype(jnp.bfloat16)
    time_part = jnp.dot(time_hidden, time_second, preferred_element_type=jnp.float32)
    time_embed = lax.all_gather(time_part, ("blk", "ulysses", "cfg"), axis=1, tiled=True)
    acted = jax.nn.silu(time_embed[None] + pooled).astype(jnp.bfloat16)
    mod_part = jnp.einsum("bpd,dc->bpc", acted, mod_weight, preferred_element_type=jnp.float32)
    mod_all = lax.all_gather(mod_part, ("blk", "ulysses", "cfg"), axis=2, tiled=True)
    own_mod = lax.dynamic_index_in_dim(mod_all, branch, 0, keepdims=False).reshape(
        prompts, 10, model_width
    )
    image_rows = img_tokens[0]
    text_rows = text_tokens[0]
    lengths = text_lengths[0]
    h_img = modulate(image_rows, own_mod[:, 0:1], own_mod[:, 1:2])
    h_txt = modulate(text_rows, own_mod[:, 4:5], own_mod[:, 3:4])
    rows_img, rows_txt = (
        lax.all_gather(h_img, "ulysses", axis=1, tiled=True),
        lax.all_gather(h_txt, "ulysses", axis=1, tiled=True),
    )
    img_span = rows_img.shape[1]
    txt_span = rows_txt.shape[1]
    img_count = 3 * prompts * img_span
    weight_piece = lax.all_gather(proj_weight, "cfg", axis=2, tiled=True)
    columns = weight_piece.shape[2]
    img_part = jnp.einsum(
        "prd,jdc->jprc", rows_img, weight_piece[0:3], preferred_element_type=jnp.float32
    )
    txt_part = jnp.einsum(
        "prd,jdc->jprc", rows_txt, weight_piece[3:5], preferred_element_type=jnp.float32
    )
    stacked_rows = jnp.concatenate(
        [img_part.reshape(-1, columns), txt_part.reshape(-1, columns)], axis=0
    )
    img_proj = stacked_rows[:img_count].reshape(3, prompts, img_span, -1)
    txt_proj = stacked_rows[img_count:].reshape(2, prompts, txt_span, -1)
    img_set, txt_set = finish(img_proj, txt_proj, qk_gain)
    inner_local = img_set.shape[3]
    head_count = inner_local // head_size
    query_heads = img_set[0].reshape(prompts, img_span, head_count, head_size)
    scale = 1.0 / math.sqrt(head_size)
    start_state = (
        jnp.full((prompts, head_count, img_span), NEG_FILL, jnp.float32),
        jnp.zeros((prompts, head_count, img_span), jnp.float32),
        jnp.zeros((prompts, img_span, head_count, head_size), jnp.float32),
    )
    text_kv = lax.all_gather(jnp.stack([txt_set[0], txt_set[1]]), "blk", axis=2, tiled=True)
    slot_usable = jnp.arange(text_kv.shape[2], dtype=jnp.int32)[None, :] < lengths[:, None]
    text_state = attend_rows(start_state, query_heads, text_kv, slot_usable, scale)
    image_kv = jnp.stack([img_set[1], img_set[2]])
    fold = make_fold(query_heads, lengths, img_span, 0, scale)
    final_state = fold(
        text_state, lax.all_gather(image_kv, "blk", axis=2, tiled=True), jnp.int32(0)
    )
    running_max, running_total, running_sum = final_state
    mixed = (running_sum / running_total.transpose(0, 2, 1)[..., None]).astype(jnp.bfloat16)
    mixed_rows = mixed.reshape(prompts, img_span, inner_local).transpose(1, 0, 2)
    out_gathered = lax.all_gather(out_weight, "cfg", axis=0, tiled=True)
    token_count = image_rows.shape[1]
    segment = mixed_rows
    attended = lax.psum_scatter(
        jnp.einsum("rpc,cd->rpd", segment, out_gathered, preferred_element_type=jnp.float32).astype(
            jnp.bfloat16
        ),
        "ulysses",
        scatter_dimension=0,
        tiled=True,
    ).astype(jnp.float32)
    attended = attended.transpose(1, 0, 2)
    residual = image_rows.astype(jnp.float32) + own_mod[:, 2:3] * attended
    feed_input = modulate(residual, own_mod[:, 7:8], own_mod[:, 8:9]).reshape(
        prompts * token_count, model_width
    )
    feed_all = lax.all_gather(feed_input, ("ulysses", "cfg"), axis=0, tiled=True)
    columns = feed_all
    pre_active = jnp.dot(
        columns,
        lax.all_gather(expand_weight, "blk", axis=0, tiled=True),
        preferred_element_type=jnp.float32,
    )
    feed_hidden = jax.nn.gelu(pre_active, approximate=True).astype(jnp.bfloat16)
    reduce_full = lax.all_gather(reduce_weight, "blk", axis=1, tiled=True)
    segment = feed_hidden
    feed_out = lax.psum_scatter(
        jnp.dot(segment, reduce_full, preferred_element_type=jnp.float32).astype(jnp.bfloat16),
        ("ulysses", "cfg"),
        scatter_dimension=0,
        tiled=True,
    ).astype(jnp.float32)
    second_residual = residual + own_mod[:, 9:10] * feed_out.reshape(
        prompts, token_count, model_width
    )
    final_rows = modulate(second_residual, own_mod[:, 6:7], own_mod[:, 5:6])
    noise = jnp.einsum("prd,dc->prc", final_rows, final_weight, preferred_element_type=jnp.float32)
    latent_channels = final_weight.shape[1] // 4
    noise_own = noise.reshape(prompts, token_count, 2, 2, latent_channels).transpose(0, 4, 2, 1, 3)
    noise_own = noise_own.reshape(prompts, latent_channels, 2, 2 * token_count)
    kept_row = lax.dynamic_slice_in_dim(noise_own, branch, 1, 2)
    sent_row = lax.dynamic_slice_in_dim(noise_own, 1 - branch, 1, 2)
    noise_pair = from_partner(sent_row, "cfg", 0)
    noise_cond = jnp.where(branch == 0, kept_row, noise_pair)
    noise_uncond = jnp.where(branch == 0, noise_pair, kept_row)
    return noise_uncond + GUIDANCE * (noise_cond - noise_uncond)


def solution(mesh):
    in_specs = (
        P("cfg", "groups", ("blk", "ulysses"), None),
        P("cfg", "groups", ("blk", "ulysses"), None),
        P("cfg", "groups"),
        P("groups"),
        P(None, "groups", None),
        P(),
        P(None, ("blk", "ulysses", "cfg")),
        P(None, ("blk", "ulysses", "cfg")),
        P(None, None, ("ulysses", "cfg")),
        P(("ulysses", "cfg"), None),
        P("blk", ("ulysses", "cfg")),
        P(("ulysses", "cfg"), "blk"),
        P(),
        P(),
    )
    out_specs = P("groups", None, ("blk", "ulysses", "cfg"), None)
    return jax.shard_map(body, mesh=mesh, in_specs=in_specs, out_specs=out_specs, check_vma=False)
```

profile of v0, /device:TPU:0, one launch (start us, length us, event | category | flops | bytes accessed | tf_op | source)
XLA Modules:
  0.0 583.4 jit_solution(9271355319539368346)
XLA Ops:
  10.2 62.9 %all-reduce = f32[2432]{0:T(1024)S(1)} all-reduce(f32[2432]{0:T(1024)S(1)} %dynamic-update-slice), channel_id=2, replica_groups=mesh['groups'=2,'blk'=4,'ulysses'=2,'cfg'=2] {'blk','ulysses','cfg'}, use_global_device_ids=true, to_apply=%add | all-reduce | flops 2432 | bytes 19456
  73.2 5.2 convolution_bitcast_fusion
  78.3 17.7 %all-gather.2 = f32[16,1520,2]{1,2,0:T(2,128)S(1)} all-gather(f32[1,1520,2]{1,2,0:T(2,128)S(1)} %convolution_bitcast_fusion), channel_id=3, replica_groups=mesh['groups'=2,'blk'=4,'ulysses'=2,'cfg'=2] {'blk','ulysses','cfg'}, dimensions={0}, use_global_device_ids=true | all-gather | bytes 206720 | tf_op jit(solution)/shard_map/all_gather | solution.py:141
  97.6 10.5 %all_gather.35 = bf16[1,128,2432]{2,1,0:T(8,128)(2,1)S(1)} all-gather(bf16[1,64,2432]{2,1,0:T(8,128)(2,1)S(1)} %fusion.53), channel_id=1, replica_groups=mesh['groups'=2,'blk'=4,'ulysses'=2,'cfg'=2] {'ulysses'}, dimensions={1}, use_global_device_ids=true | all-gather | bytes 933888 | tf_op jit(solution)/shard_map/all_gather | solution.py:151
  108.2 6.5 %fusion.21 = f32[3,1,128,1024]{3,2,0,1:T(8,128)S(1)} fusion(bf16[5,2432,1024]{2,1,0:T(8,128)(2,1)} %all-gather.10.cloned.1.call-done, bf16[1,128,2432]{2,1,0:T(8,128)(2,1)S(1)} %all_gather.35), kind=kOutput, calls=%fused_computation.26 | convolution fusion | flops 1912602624 | bytes 17137664 | tf_op jit(solution)/shard_map/prd,jdc->jprc/dot_general | solution.py:159
  116.0 2.0 slice_multiply_fusion.2
  120.9 4.9 all_gather.37
  125.8 5.3 fusion.32
  131.7 15.8 %all_gather.38 = bf16[2,1,48,1024]{3,0,1,2:T(2,128)(2,1)S(1)} all-gather(bf16[2,1,12,1024]{3,0,1,2:T(2,128)(2,1)S(1)} %copy.64), channel_id=1, replica_groups=mesh['groups'=2,'blk'=4,'ulysses'=2,'cfg'=2] {'blk'}, dimensions={2}, use_global_device_ids=true | all-gather | bytes 245760 | tf_op jit(solution)/shard_map/all_gather | solution.py:180
  149.4 16.9 %all-gather.12.cloned.1.call-done = bf16[2,1,512,1024]{3,2,0,1:T(8,128)(2,1)} async-done(((bf16[2,1,128,1024]{3,2,0,1:T(8,128)(2,1)}), bf16[2,1,512,1024]{3,2,0,1:T(8,128)(2,1)}) %all-gather.12.cloned.1.call-update) | async-done | bytes 2097168 | tf_op jit(solution)/shard_map/all_gather | solution.py:186
  166.4 3.1 fusion.107
  169.4 1.5 copy.69
  170.9 2.3 copy.70
  176.7 4.8 all-gather.14.cloned.1.call-done
  181.6 4.1 fusion.4
  186.9 15.8 %reduce-scatter.3.cloned.1.call-done = bf16[64,1,2432]{2,0,1:T(8,128)(2,1)} async-done(((bf16[128,1,2432]{2,0,1:T(8,128)(2,1)}), bf16[64,1,2432]{2,0,1:T(8,128)(2,1)}) %reduce-scatter.3.cloned.1.call-update) | async-done | bytes 311312 | tf_op jit(solution)/shard_map/reduce_scatter | solution.py:194
  205.2 1.9 add_convert_fusion.1
  207.4 151.8 %all-gather.18.cloned.1.call-done = bf16[2432,1792]{1,0:T(8,128)(2,1)} async-done(((bf16[608,1792]{1,0:T(8,128)(2,1)}), bf16[2432,1792]{1,0:T(8,128)(2,1)}) %all-gather.18.cloned.1.call-update) | async-done | bytes 8716304 | tf_op jit(solution)/shard_map/all_gather | solution.py:211
  359.2 154.6 %all-gather.20.cloned.1.call-done = bf16[1792,2432]{0,1:T(8,128)(2,1)} async-done(((bf16[1792,608]{0,1:T(8,128)(2,1)}), bf16[1792,2432]{0,1:T(8,128)(2,1)}) %all-gather.20.cloned.1.call-update) | async-done | bytes 8716304 | tf_op jit(solution)/shard_map/all_gather | solution.py:215
  513.8 17.6 %all-gather.16.cloned.1.call-done = bf16[256,2432]{1,0:T(8,128)(2,1)} async-done(((bf16[64,2432]{1,0:T(8,128)(2,1)}), bf16[256,2432]{1,0:T(8,128)(2,1)}) %all-gather.16.cloned.1.call-update) | async-done | bytes 1245200 | tf_op jit(solution)/shard_map/all_gather | solution.py:207
  531.4 13.0 %convolution_convert_fusion = bf16[256,2432]{1,0:T(8,128)(2,1)} fusion(bf16[1792,2432]{0,1:T(8,128)(2,1)} %all-gather.20.cloned.1.call-done, bf16[256,2432]{1,0:T(8,128)(2,1)} %all-gather.16.cloned.1.call-done, bf16[2432,1792]{1,0:T(8,128)(2,1)} %all-gather.18.cloned.1.call-done), kind=kOutput, calls=%fused_computation.6 | convolution fusion | flops 4467490816 | bytes 19922944 | tf_op jit(solution)/shard_map/dot_general | solution.py:218
  544.4 26.2 %reduce-scatter.5.cloned.1.call-done = bf16[64,2432]{1,0:T(8,128)(2,1)} async-done(((bf16[256,2432]{1,0:T(8,128)(2,1)}), bf16[64,2432]{1,0:T(8,128)(2,1)}) %reduce-scatter.5.cloned.1.call-update) | async-done | bytes 311312 | tf_op jit(solution)/shard_map/reduce_scatter | solution.py:217
  571.8 1.3 multiply_reduce_fusion
  573.1 1.4 convolution_bitcast_fusion.2
  (121 shorter events, 20.4 us)
Async XLA Ops:
  6.5 1.5 copy-start
  6.5 1.9 copy-start.11
  6.5 3.1 copy-start.6
  6.5 66.5 %copy-start.8 = (f32[2,1,2432]{2,1,0:T(1,128)S(1)}, f32[2,1,2432]{2,1,0:T(1,128)}, u32[]{:S(2)}) copy-start(f32[2,1,2432]{2,1,0:T(1,128)} %param.18) | copy-start | bytes 58372
  6.5 101.6 %all-gather.10.cloned.1.call-start = ((), (), s32[]{:S(2)}) async-start(), calls=%async_computation.2 | async-start | bytes 37355520 | tf_op jit(solution)/shard_map/all_gather | solution.py:157
  7.3 159.1 %all-gather.12.cloned.1.call-start = ((), (), s32[]{:S(2)}) async-start(), calls=%async_computation.3 | async-start | bytes 2621440 | tf_op jit(solution)/shard_map/all_gather | solution.py:186
  73.1 23.5 %copy-start.9 = (f32[3,64]{1,0:T(4,128)S(1)}, f32[3,64]{1,0:T(4,128)}, u32[]{:S(2)}) copy-start(f32[3,64]{1,0:T(4,128)} %param.26) | copy-start | bytes 2308
  73.1 23.6 %copy-start.2 = (bf16[1,1,64,2432]{3,2,1,0:T(8,128)(2,1)S(1)}, bf16[1,1,64,2432]{3,2,1,0:T(8,128)(2,1)}, u32[]{:S(2)}) copy-start(bf16[1,1,64,2432]{3,2,1,0:T(8,128)(2,1)} %param.14) | copy-start | bytes 933892
  115.0 4.7 copy-start.7
  118.9 62.7 %all-gather.14.cloned.1.call-start = ((), (), s32[]{:S(2)}) async-start(), calls=%async_computation.4 | async-start | bytes 7471104 | tf_op jit(solution)/shard_map/all_gather | solution.py:191
  119.6 83.2 %reduce-scatter.3.cloned.1.call-start = ((), (), s32[]{:S(2)}) async-start(), calls=%async_computation.5 | async-start | bytes 933888 | tf_op jit(solution)/shard_map/reduce_scatter | solution.py:194
  125.8 22.6 %copy-start.4 = (f32[1,1,128,1024]{3,2,0,1:T(8,128)S(1)}, f32[1,1,128,1024]{3,2,0,1:T(8,128)}, u32[]{:S(2)}) copy-start(f32[1,1,128,1024]{3,2,0,1:T(8,128)} %get-tuple-element.21) | copy-start | bytes 1572868
  174.1 1.5 copy-start.5
  185.7 173.5 %all-gather.18.cloned.1.call-start = ((), (), s32[]{:S(2)}) async-start(), calls=%async_computation.7 | async-start | bytes 10895360 | tf_op jit(solution)/shard_map/all_gather | solution.py:211
  186.3 327.5 %all-gather.20.cloned.1.call-start = ((), (), s32[]{:S(2)}) async-start(), calls=%async_computation.8 | async-start | bytes 10895360 | tf_op jit(solution)/shard_map/all_gather | solution.py:215
  186.9 344.5 %all-gather.16.cloned.1.call-start = ((), (), s32[]{:S(2)}) async-start(), calls=%async_computation.6 | async-start | bytes 1556480 | tf_op jit(solution)/shard_map/all_gather | solution.py:207
  207.1 363.5 %copy-start.3 = (bf16[64,1,2432]{2,0,1:T(8,128)(2,1)S(1)}, bf16[64,1,2432]{2,0,1:T(8,128)(2,1)}, u32[]{:S(2)}) copy-start(bf16[64,1,2432]{2,0,1:T(8,128)(2,1)} %reduce-scatter.3.cloned.1.call-done) | copy-start | bytes 933892
  207.1 366.0 %copy-start.10 = (bf16[2432,64]{0,1:T(8,128)(2,1)S(1)}, bf16[2432,64]{0,1:T(8,128)(2,1)}, u32[]{:S(2)}) copy-start(bf16[2432,64]{0,1:T(8,128)(2,1)} %param.27) | copy-start | bytes 933892
  207.1 363.4 %reduce-scatter.5.cloned.1.call-start = ((), (), s32[]{:S(2)}) async-start(), calls=%async_computation.9 | async-start | bytes 1556480 | tf_op jit(solution)/shard_map/reduce_scatter | solution.py:217
  531.4 45.1 %copy-start.1 = (bf16[256,2432]{1,0:T(8,128)(2,1)S(1)}, bf16[256,2432]{1,0:T(8,128)(2,1)}, u32[]{:S(2)}) copy-start(bf16[256,2432]{1,0:T(8,128)(2,1)} %param.19) | copy-start | bytes 3735556
  574.7 1.2 collective-permute-start
Sparse Core Ops, SparseCore 0:
  8.9 42.6 all-gather.9
  119.0 47.3 all-gather.11
  167.9 13.6 all-gather.13
  185.8 16.8 reduce-scatter.2
  204.2 154.9 all-gather.17
  360.6 153.1 all-gather.19
  515.4 15.9 all-gather.15
  544.5 26.0 reduce-scatter.4
where the time goes:
time: 584 us; the launch traced here: 583 us
  waiting for transfers between devices  391 us (67%)
  blocking collectives  112 us (19%)
  matrix products  38.7 us (7%)
  between operations  16 us (3%)
  other arithmetic  13.3 us (2%)
  local copies, waits for them, and re-layouts  11.8 us (2%)
    all_gather x1, waiting for transfers between devices, body(): reduce_full = lax.all_gather(reduce_weight, 'blk', axis=1, tiled=True)  155 us
    all_gather x1, waiting for transfers between devices, body(): lax.all_gather(expand_weight, 'blk', axis=0, tiled=True)  152 us
    unnamed x1, blocking collectives  62.9 us
    reduce_scatter x1, waiting for transfers between devices, body(): lax.psum_scatter(jnp.dot(segment, reduce_full, preferred_element_type=jnp...  26.2 us
    all_gather x1, blocking collectives, body(): lax.all_gather(mod_part, ('blk', 'ulysses', 'cfg'), axis=2, tiled=True)  17.7 us
    all_gather x1, waiting for transfers between devices, body(): lax.all_gather(feed_input, ('ulysses', 'cfg'), axis=0, tiled=True)  17.6 us
    all_gather x1, waiting for transfers between devices, body(): lax.all_gather(image_kv, 'blk', axis=2, tiled=True)  16.9 us
    reduce_scatter x1, waiting for transfers between devices, body(): lax.psum_scatter(jnp.einsum('rpc,cd->rpd', segment, out_gathered, preferr...  15.8 us
  transfers between devices with their start and end apart: 9, of which 8 were waited for; matrix products, arithmetic and copies ran while one was open for 5% of the time, Pallas kernels for 0%

commit v1 on v0

--- a/solution.py
+++ b/solution.py
@@ -212,7 +212,12 @@
         preferred_element_type=jnp.float32,
     )
     feed_hidden = jax.nn.gelu(pre_active, approximate=True).astype(jnp.bfloat16)
-    reduce_full = lax.all_gather(reduce_weight, "blk", axis=1, tiled=True)
+    ring = [reduce_weight]
+    for hop in range(3):
+        ring.append(lax.ppermute(ring[-1], "blk", [(dev, (dev + 1) % 4) for dev in range(4)]))
+    reduce_full = jnp.roll(
+        jnp.concatenate(ring[::-1], axis=1), (lax.axis_index("blk") + 1) * ring[0].shape[1], axis=1
+    )
     segment = feed_hidden
     feed_out = lax.psum_scatter(
         jnp.dot(segment, reduce_full, preferred_element_type=jnp.float32).astype(jnp.bfloat16),

time: 584 us -> 552 us (0.945)
  waiting for transfers between devices: 391 us -> 265 us
  starting transfers between devices: 0.57 us -> 72.7 us
  local copies, waits for them, and re-layouts: 11.8 us -> 33.5 us
    ppermute x0 -> x3, waiting for transfers between devices: none -> 215 us  [body(): lax.ppermute(ring[-1], 'blk', [(dev, (dev + 1) % 4) for dev in range(4)])]
    all_gather x1 -> x0, waiting for transfers between devices: 155 us -> none  [body(): reduce_full = lax.all_gather(reduce_weight, 'blk', axis=1, tiled=True)]
    all_gather x1, waiting for transfers between devices: 152 us -> 0.01 us  [body(): lax.all_gather(expand_weight, 'blk', axis=0, tiled=True)]
    ppermute x0 -> x3, starting transfers between devices: none -> 72.2 us  [body(): lax.ppermute(ring[-1], 'blk', [(dev, (dev + 1) % 4) for dev in range(4)])]
    unnamed x31 -> x44, local copies, waits for them, and re-layouts: 1.48 us -> 21.8 us
    all_gather x1, waiting for transfers between devices: 17.6 us -> 0.01 us  [body(): lax.all_gather(feed_input, ('ulysses', 'cfg'), axis=0, tiled=True)]
    reduce_scatter x1, waiting for transfers between devices: 15.8 us -> 0.01 us  [body(): lax.psum_scatter(jnp.einsum('rpc,cd->rpd', segment, out_gathered, preferr...]
  transfers between devices with their start and end apart: 9 -> 11, of which waited for: 8 -> 7; matrix products, arithmetic and copies ran while one was open for 5% -> 9% of each run, Pallas kernels for 0% -> 0%
where the time goes in v1:
time: 552 us; the launch traced here: 551 us
  waiting for transfers between devices  265 us (48%)
  blocking collectives  112 us (20%)
  starting transfers between devices  72.7 us (13%)
  matrix products  38.7 us (7%)
  local copies, waits for them, and re-layouts  33.5 us (6%)
  between operations  16 us (3%)
  other arithmetic  13.3 us (2%)
    ppermute x3, waiting for transfers between devices, body(): lax.ppermute(ring[-1], 'blk', [(dev, (dev + 1) % 4) for dev in range(4)])  215 us
    ppermute x3, starting transfers between devices, body(): lax.ppermute(ring[-1], 'blk', [(dev, (dev + 1) % 4) for dev in range(4)])  72.2 us
    unnamed x1, blocking collectives  62.9 us
    reduce_scatter x1, waiting for transfers between devices, body(): lax.psum_scatter(jnp.dot(segment, reduce_full, preferred_element_type=jnp...  25.8 us
    unnamed x44, local copies, waits for them, and re-layouts  21.8 us
    all_gather x1, blocking collectives, body(): lax.all_gather(mod_part, ('blk', 'ulysses', 'cfg'), axis=2, tiled=True)  17.7 us
    all_gather x1, waiting for transfers between devices, body(): lax.all_gather(image_kv, 'blk', axis=2, tiled=True)  17.1 us
    all_gather x1, blocking collectives, body(): lax.all_gather(jnp.stack([txt_set[0], txt_set[1]]), 'blk', axis=2, tiled=...  15.7 us
  transfers between devices with their start and end apart: 11, of which 7 were waited for; matrix products, arithmetic and copies ran while one was open for 9% of the time, Pallas kernels for 0%

profile of v1, /device:TPU:0, one launch (start us, length us, event | category | flops | bytes accessed | tf_op | source)
XLA Modules:
  0.0 551.3 jit_solution(18010061782395105779)
XLA Ops:
  10.2 62.9 %all-reduce = f32[2432]{0:T(1024)S(1)} all-reduce(f32[2432]{0:T(1024)S(1)} %dynamic-update-slice), channel_id=2, replica_groups=mesh['groups'=2,'blk'=4,'ulysses'=2,'cfg'=2] {'blk','ulysses','cfg'}, use_global_device_ids=true, to_apply=%add | all-reduce | flops 2432 | bytes 19456
  73.2 5.2 convolution_bitcast_fusion
  78.3 17.7 %all-gather.2 = f32[16,1520,2]{1,2,0:T(2,128)S(1)} all-gather(f32[1,1520,2]{1,2,0:T(2,128)S(1)} %convolution_bitcast_fusion), channel_id=3, replica_groups=mesh['groups'=2,'blk'=4,'ulysses'=2,'cfg'=2] {'blk','ulysses','cfg'}, dimensions={0}, use_global_device_ids=true | all-gather | bytes 206720 | tf_op jit(solution)/shard_map/all_gather | solution.py:141
  97.6 10.5 %all_gather.32 = bf16[1,128,2432]{2,1,0:T(8,128)(2,1)S(1)} all-gather(bf16[1,64,2432]{2,1,0:T(8,128)(2,1)S(1)} %fusion.58), channel_id=1, replica_groups=mesh['groups'=2,'blk'=4,'ulysses'=2,'cfg'=2] {'ulysses'}, dimensions={1}, use_global_device_ids=true | all-gather | bytes 933888 | tf_op jit(solution)/shard_map/all_gather | solution.py:151
  108.2 6.5 %fusion.26 = f32[3,1,128,1024]{3,2,0,1:T(8,128)S(1)} fusion(bf16[5,2432,1024]{2,1,0:T(8,128)(2,1)} %all-gather.9.cloned.1.call-done, bf16[1,128,2432]{2,1,0:T(8,128)(2,1)S(1)} %all_gather.32), kind=kOutput, calls=%fused_computation.28 | convolution fusion | flops 1912602624 | bytes 17137664 | tf_op jit(solution)/shard_map/prd,jdc->jprc/dot_general | solution.py:159
  120.9 4.8 all_gather.34
  126.3 5.2 fusion.37
  132.0 15.7 %all_gather.35 = bf16[2,1,48,1024]{3,0,1,2:T(2,128)(2,1)S(1)} all-gather(bf16[2,1,12,1024]{3,0,1,2:T(2,128)(2,1)S(1)} %copy.64), channel_id=1, replica_groups=mesh['groups'=2,'blk'=4,'ulysses'=2,'cfg'=2] {'blk'}, dimensions={2}, use_global_device_ids=true | all-gather | bytes 245760 | tf_op jit(solution)/shard_map/all_gather | solution.py:180
  149.2 17.1 %all-gather.11.cloned.1.call-done = bf16[2,1,512,1024]{3,2,0,1:T(8,128)(2,1)} async-done(((bf16[2,1,128,1024]{3,2,0,1:T(8,128)(2,1)}), bf16[2,1,512,1024]{3,2,0,1:T(8,128)(2,1)}) %all-gather.11.cloned.1.call-update) | async-done | bytes 2097168 | tf_op jit(solution)/shard_map/all_gather | solution.py:186
  166.3 3.1 fusion.113
  176.7 4.8 all-gather.13.cloned.1.call-done
  181.5 4.1 fusion.9
  188.2 70.3 %collective-permute-done = bf16[1792,608]{0,1:T(8,128)(2,1)S(1)} collective-permute-done((bf16[1792,608]{0,1:T(8,128)(2,1)}, bf16[1792,608]{0,1:T(8,128)(2,1)S(1)}, u32[]{:S(2)}, u32[]{:S(2)}) %collective-permute-start) | collective-permute-done | bytes 2179104 | tf_op jit(solution)/shard_map/ppermute | solution.py:217
  259.9 23.1 %collective-permute-start.1 = (bf16[1792,608]{0,1:T(8,128)(2,1)S(1)}, bf16[1792,608]{0,1:T(8,128)(2,1)}, u32[]{:S(2)}, u32[]{:S(2)}) collective-permute-start(bf16[1792,608]{0,1:T(8,128)(2,1)S(1)} %collective-permute-done), channel_id=1, source_target_pairs={{0,4},{4,8},{8,12},{12,0},{1,5},{5,9},{9,13},{13,1},{2,6},{6,10},{... | collective-permute-start | bytes 6537224 | tf_op jit(solution)/shard_map/ppermute | solution.py:217
  282.9 93.5 %collective-permute-done.1 = bf16[1792,608]{0,1:T(8,128)(2,1)} collective-permute-done((bf16[1792,608]{0,1:T(8,128)(2,1)S(1)}, bf16[1792,608]{0,1:T(8,128)(2,1)}, u32[]{:S(2)}, u32[]{:S(2)}) %collective-permute-start.1) | collective-permute-done | bytes 2179104 | tf_op jit(solution)/shard_map/ppermute | solution.py:217
  376.5 47.3 %collective-permute-start.2 = (bf16[1792,608]{0,1:T(8,128)(2,1)}, bf16[1792,608]{0,1:T(8,128)(2,1)}, u32[]{:S(2)}, u32[]{:S(2)}) collective-permute-start(bf16[1792,608]{0,1:T(8,128)(2,1)} %collective-permute-done.1), channel_id=1, source_target_pairs={{0,4},{4,8},{8,12},{12,0},{1,5},{5,9},{9,13},{13,1},{2,6},{6,10},{... | collective-permute-start | bytes 6537224 | tf_op jit(solution)/shard_map/ppermute | solution.py:217
  423.7 50.7 %collective-permute-done.2 = bf16[1792,608]{0,1:T(8,128)(2,1)} collective-permute-done((bf16[1792,608]{0,1:T(8,128)(2,1)}, bf16[1792,608]{0,1:T(8,128)(2,1)}, u32[]{:S(2)}, u32[]{:S(2)}) %collective-permute-start.2) | collective-permute-done | bytes 2179104 | tf_op jit(solution)/shard_map/ppermute | solution.py:217
  474.5 3.1 constant_dynamic-update-slice_fusion.7
  482.2 3.2 constant_dynamic-update-slice_fusion.6
  485.5 3.1 constant_dynamic-update-slice_fusion.5
  490.1 3.3 constant_dynamic-update-slice_fusion.3
  493.4 3.1 constant_dynamic-update-slice_fusion.2
  499.5 13.1 %fusion.6 = bf16[256,2432]{1,0:T(8,128)(2,1)} fusion(bf16[1792,4864]{0,1:T(8,128)(2,1)} %constant_dynamic-update-slice_fusion, s32[]{:T(128)S(6)} %select_n.71, bf16[256,2432]{1,0:T(8,128)(2,1)} %all-gather.15.cloned.1.call-done, bf16[2432,1792]{1,0:T(8,128)(2,1)} %all-gather.17.cloned.1.call-done), kind=kOutput, calls=%fused_computation.8 | convolution fusion | flops 4467490816 | bytes 19922948 | tf_op jit(solution)/shard_map/dot_general | solution.py:223
  512.7 25.8 %reduce-scatter.5.cloned.1.call-done = bf16[64,2432]{1,0:T(8,128)(2,1)} async-done(((bf16[256,2432]{1,0:T(8,128)(2,1)}), bf16[64,2432]{1,0:T(8,128)(2,1)}) %reduce-scatter.5.cloned.1.call-update) | async-done | bytes 311312 | tf_op jit(solution)/shard_map/reduce_scatter | solution.py:222
  (138 shorter events, 37.8 us)
Async XLA Ops:
  6.5 1.9 copy-start.14
  6.5 3.1 copy-start.9
  6.5 66.5 %copy-start.11 = (f32[2,1,2432]{2,1,0:T(1,128)S(1)}, f32[2,1,2432]{2,1,0:T(1,128)}, u32[]{:S(2)}) copy-start(f32[2,1,2432]{2,1,0:T(1,128)} %param.18) | copy-start | bytes 58372
  6.5 101.6 %all-gather.9.cloned.1.call-start = ((), (), s32[]{:S(2)}) async-start(), calls=%async_computation.2 | async-start | bytes 37355520 | tf_op jit(solution)/shard_map/all_gather | solution.py:157
  7.3 159.1 %all-gather.11.cloned.1.call-start = ((), (), s32[]{:S(2)}) async-start(), calls=%async_computation.3 | async-start | bytes 2621440 | tf_op jit(solution)/shard_map/all_gather | solution.py:186
  73.1 23.5 %copy-start.12 = (f32[3,64]{1,0:T(4,128)S(1)}, f32[3,64]{1,0:T(4,128)}, u32[]{:S(2)}) copy-start(f32[3,64]{1,0:T(4,128)} %param.26) | copy-start | bytes 2308
  73.1 23.6 %copy-start.2 = (bf16[1,1,64,2432]{3,2,1,0:T(8,128)(2,1)S(1)}, bf16[1,1,64,2432]{3,2,1,0:T(8,128)(2,1)}, u32[]{:S(2)}) copy-start(bf16[1,1,64,2432]{3,2,1,0:T(8,128)(2,1)} %param.14) | copy-start | bytes 933892
  115.0 4.7 copy-start.10
  118.0 7.8 %copy-start.7 = (f32[1,1,128,1024]{3,2,0,1:T(8,128)S(1)}, f32[1,1,128,1024]{3,2,0,1:T(8,128)}, u32[]{:S(2)}) copy-start(f32[1,1,128,1024]{3,2,0,1:T(8,128)} %get-tuple-element.21) | copy-start | bytes 1572868
  118.9 62.7 %all-gather.13.cloned.1.call-start = ((), (), s32[]{:S(2)}) async-start(), calls=%async_computation.4 | async-start | bytes 7471104 | tf_op jit(solution)/shard_map/all_gather | solution.py:191
  119.6 358.0 %reduce-scatter.3.cloned.1.call-start = ((), (), s32[]{:S(2)}) async-start(), calls=%async_computation.5 | async-start | bytes 933888 | tf_op jit(solution)/shard_map/reduce_scatter | solution.py:194
  174.1 1.5 copy-start.8
  185.7 313.8 %all-gather.17.cloned.1.call-start = ((), (), s32[]{:S(2)}) async-start(), calls=%async_computation.7 | async-start | bytes 10895360 | tf_op jit(solution)/shard_map/all_gather | solution.py:211
  186.3 313.2 %all-gather.15.cloned.1.call-start = ((), (), s32[]{:S(2)}) async-start(), calls=%async_computation.6 | async-start | bytes 1556480 | tf_op jit(solution)/shard_map/all_gather | solution.py:207
  186.4 72.1 %collective-permute-start = (bf16[1792,608]{0,1:T(8,128)(2,1)}, bf16[1792,608]{0,1:T(8,128)(2,1)S(1)}, u32[]{:S(2)}, u32[]{:S(2)}) collective-permute-start(bf16[1792,608]{0,1:T(8,128)(2,1)} %param.25), channel_id=1, source_target_pairs={{0,4},{4,8},{8,12},{12,0},{1,5},{5,9},{9,13},{13,1},{2,6},{6,10},{... | collective-permute-start | bytes 6537224 | tf_op jit(solution)/shard_map/ppermute | solution.py:217
  259.9 116.6 %collective-permute-start.1 = (bf16[1792,608]{0,1:T(8,128)(2,1)S(1)}, bf16[1792,608]{0,1:T(8,128)(2,1)}, u32[]{:S(2)}, u32[]{:S(2)}) collective-permute-start(bf16[1792,608]{0,1:T(8,128)(2,1)S(1)} %collective-permute-done), channel_id=1, source_target_pairs={{0,4},{4,8},{8,12},{12,0},{1,5},{5,9},{9,13},{13,1},{2,6},{6,10},{... | collective-permute-start | bytes 6537224 | tf_op jit(solution)/shard_map/ppermute | solution.py:217
  376.5 98.0 %collective-permute-start.2 = (bf16[1792,608]{0,1:T(8,128)(2,1)}, bf16[1792,608]{0,1:T(8,128)(2,1)}, u32[]{:S(2)}, u32[]{:S(2)}) collective-permute-start(bf16[1792,608]{0,1:T(8,128)(2,1)} %collective-permute-done.1), channel_id=1, source_target_pairs={{0,4},{4,8},{8,12},{12,0},{1,5},{5,9},{9,13},{13,1},{2,6},{6,10},{... | collective-permute-start | bytes 6537224 | tf_op jit(solution)/shard_map/ppermute | solution.py:217
  481.9 56.6 %reduce-scatter.5.cloned.1.call-start = ((), (), s32[]{:S(2)}) async-start(), calls=%async_computation.8 | async-start | bytes 1556480 | tf_op jit(solution)/shard_map/reduce_scatter | solution.py:222
  482.2 6.4 %copy-start.3 = (bf16[1792,608]{0,1:T(8,128)(2,1)S(1)}, bf16[1792,608]{0,1:T(8,128)(2,1)}, u32[]{:S(2)}) copy-start(bf16[1792,608]{0,1:T(8,128)(2,1)} %param.25) | copy-start | bytes 6537220
  490.1 6.5 %copy-start.5 = (bf16[1792,608]{0,1:T(8,128)(2,1)S(1)}, bf16[1792,608]{0,1:T(8,128)(2,1)}, u32[]{:S(2)}) copy-start(bf16[1792,608]{0,1:T(8,128)(2,1)} %copy-done.4) | copy-start | bytes 6537220
  499.5 39.0 %copy-start.6 = (bf16[64,1,2432]{2,0,1:T(8,128)(2,1)S(1)}, bf16[64,1,2432]{2,0,1:T(8,128)(2,1)}, u32[]{:S(2)}) copy-start(bf16[64,1,2432]{2,0,1:T(8,128)(2,1)} %reduce-scatter.3.cloned.1.call-done) | copy-start | bytes 933892
  499.5 41.5 %copy-start.13 = (bf16[2432,64]{0,1:T(8,128)(2,1)S(1)}, bf16[2432,64]{0,1:T(8,128)(2,1)}, u32[]{:S(2)}) copy-start(bf16[2432,64]{0,1:T(8,128)(2,1)} %param.27) | copy-start | bytes 933892
  499.5 44.9 %copy-start.1 = (bf16[256,2432]{1,0:T(8,128)(2,1)S(1)}, bf16[256,2432]{1,0:T(8,128)(2,1)}, u32[]{:S(2)}) copy-start(bf16[256,2432]{1,0:T(8,128)(2,1)} %param.19) | copy-start | bytes 3735556
  542.6 1.2 collective-permute-start.3
  (2 other events, 2.9 us)
Sparse Core Ops, SparseCore 0:
  8.9 42.6 all-gather.8
  119.0 47.3 all-gather.10
  167.9 13.6 all-gather.12
  185.8 16.8 reduce-scatter.2
  204.2 221.2 all-gather.16
  482.1 17.1 all-gather.14
  512.8 25.6 reduce-scatter.4
